TPU v7x, 32 devices: a whole 2x2x4 slice. The times are simulated.
32 devices in a mesh: row: 4 (over y, x), col: 8 (over z, core).
Axes of the slice: x: 2, y: 2, z: 4, core: 2. Of those that a mesh axis runs over, the one named last changes fastest.
Arguments:
- voltages: bfloat16 [4096, 32, 2, 256], P(('col', 'row')), may hold values from -6 to 6
- auto_prev: float32 [32, 4096], P('row', 'col'), may hold values from 0.5 to 8
- station_order: int32 [4096], replicated, may hold values from 0 to 4095, each once
Outputs:
- visibilities: bfloat16 [32, 5, 4096, 1024], P('row', None, 'col')
Inputs may be any that keep to these rules, and one draw needn't show every extreme that they name: `station_order`: a permutation of the block positions.
All inputs are finite; a program needn't handle non-finite values.
Results may differ from a plain program's by a relative error of at most 0.001.
Values may be sent and summed in bfloat16 or wider, within the bound.
No kernel may reach another device: no remote copies, remote signals or barrier semaphores. Data moves between devices by JAX's collectives and lax.ppermute only.
A program may use at most 192 MiB of HBM per device.

v0:
```python
import jax
import jax.numpy as jnp
from jax import lax
from jax.experimental import pallas as pl
from jax.experimental.pallas import tpu as pltpu
from jax.sharding import PartitionSpec as P


LANES = 128
VMEM_LIMIT = 253 * 256 * 1024


def swap_with(value, axis, distance):
    count = lax.axis_size(axis)
    return lax.ppermute(value, axis, [(i, i ^ distance) for i in range(count)])


def from_behind(value, axis):
    count = lax.axis_size(axis)
    return lax.ppermute(value, axis, [(i, (i + 1) % count) for i in range(count)])


def rows_distance(turn, parity, rows):
    if parity == 1 and turn in (1, 2) and rows > 2:
        return 3 - turn
    return turn


def traded(value, turn):
    rows, cols = lax.axis_size("row"), lax.axis_size("col")
    pairs = []
    for row in range(rows):
        for col in range(cols):
            other = row ^ rows_distance(turn, col % 2, rows)
            pairs.append((row * cols + col, other * cols + col))
    return lax.ppermute(value, ("row", "col"), pairs)


def gather_piece(group_ref, voltages_ref, out_ref):
    stations, chan_count, parts, samples = voltages_ref.shape
    for chan in range(chan_count):
        out_ref[chan] = voltages_ref[:, chan, :, :].reshape(stations, parts * samples)


def piece_of(voltages, group, chan_count):
    stations, _, parts, samples = voltages.shape
    steps = 2 if stations % 32 == 0 else 1
    some = stations // steps
    return pl.pallas_call(
        gather_piece,
        grid_spec=pltpu.PrefetchScalarGridSpec(
            num_scalar_prefetch=1,
            grid=(steps,),
            in_specs=[
                pl.BlockSpec((some, chan_count, parts, samples), lambda i, at: (i, at[0], 0, 0))
            ],
            out_specs=pl.BlockSpec((chan_count, some, parts * samples), lambda i, at: (0, i, 0)),
        ),
        out_shape=jax.ShapeDtypeStruct((chan_count, stations, parts * samples), voltages.dtype),
    )(group, voltages)


def turned_of(rows):
    half = rows.shape[-1] // 2
    return jnp.concatenate([-rows[:, half:], rows[:, :half]], axis=-1)


def gram_of(left, right):
    return lax.dot_general(
        left, right, (((1,), (1,)), ((), ())), preferred_element_type=jnp.float32
    )


def tiles_kernel(count, chosen, offset, column_start, slots, places_ref, *refs):
    own, partner = refs[:count], refs[count : count + len(chosen)]
    row_scale_ref, column_scale_ref = refs[count + len(chosen) : count + len(chosen) + 2]
    out_ref, left_ref, right_ref, rows_ref, columns_ref, stage_ref, loaded, read, sent = refs[-9:]
    chan_count, height, _ = own[0].shape
    block_size = height * count
    whole = len(chosen) == count
    width = height * len(chosen)
    first_column = column_start
    if not whole:
        first_column = pl.multiple_of(column_start + places_ref[count + chosen[0]] * height, LANES)

    def loads(chan):
        result = []
        for index, ref in enumerate([*own, *partner]):
            to_ref = left_ref if index < count else right_ref
            top = 0
            if index < count or whole:
                top = pl.multiple_of(places_ref[index] * height, height)
            result.append((ref.at[chan], to_ref.at[chan, pl.ds(top, height)]))
        result.append((row_scale_ref.at[chan], rows_ref.at[chan]))
        return [
            pltpu.make_async_copy(source, target, loaded.at[chan, index])
            for index, (source, target) in enumerate(result)
        ]

    def sends(chan):
        slot = chan % slots
        if whole:
            return [pltpu.make_async_copy(stage_ref.at[slot], out_ref.at[chan, offset], sent.at[slot, 0])]
        result = []
        for part in range(2):
            column = part * block_size + places_ref[count + chosen[0]] * height
            column = pl.multiple_of(column, LANES)
            result.append(
                pltpu.make_async_copy(
                    stage_ref.at[slot, :, pl.ds(part * height, height)],
                    out_ref.at[chan, offset, :, pl.ds(column, height)],
                    sent.at[slot, part],
                )
            )
        return result

    columns_load = pltpu.make_async_copy(
        column_scale_ref.at[:, :, pl.ds(first_column, width)], columns_ref, read
    )
    columns_load.start()

    def start_loads(chan, carry):
        for copy in loads(chan):
            copy.start()
        return carry

    lax.fori_loop(0, chan_count, start_loads, 0)
    columns_load.wait()

    def one_channel(chan, carry):
        slot = chan % slots
        for copy in loads(chan):
            copy.wait()
        if slots < chan_count:

            @pl.when(chan >= slots)
            def _():
                for copy in sends(chan - slots):
                    copy.wait()

        left = left_ref[chan]
        row_scale = rows_ref[chan]
        for lane in range(0, width, LANES):
            right = right_ref[chan, lane : lane + LANES, :]
            gram = gram_of(left, jnp.concatenate([right, turned_of(right)], axis=0))
            scale = columns_ref[chan, :, lane : lane + LANES]
            for part in range(2):
                tile = gram[:, part * LANES : (part + 1) * LANES] * row_scale * scale
                column = part * width + lane
                stage_ref[slot, :, column : column + LANES] = tile.astype(stage_ref.dtype)
        for copy in sends(chan):
            copy.start()
        return carry

    lax.fori_loop(0, chan_count, one_channel, 0)

    def drain(chan, carry):
        for copy in sends(chan):
            copy.wait()
        return carry

    lax.fori_loop(chan_count - slots, chan_count, drain, 0)


def tile_call(out, shape, places, own, partner, row_scale, column_scale, offset, chosen):
    chan_count, offsets, block_size, _ = shape
    count, (_, height, depth) = len(own), own[0].shape
    slots = 2 if len(chosen) == count else chan_count
    width = height * len(chosen)
    operands = [*own, *[partner[piece] for piece in chosen], row_scale, column_scale]
    aliases = {}
    if out is not None:
        aliases = {1 + len(operands): 0}
        operands.append(out)
    in_specs = [pl.BlockSpec(memory_space=pltpu.SMEM)]
    in_specs += [pl.BlockSpec(memory_space=pl.ANY)] * len(operands)
    column_start = (offsets - 1 - offset) * block_size

    def body(*refs):
        tiles_kernel(count, chosen, offset, column_start, slots, *refs)

    return pl.pallas_call(
        body,
        in_specs=in_specs,
        out_specs=pl.BlockSpec(memory_space=pl.ANY),
        out_shape=jax.ShapeDtypeStruct(shape, jnp.bfloat16),
        scratch_shapes=[
            pltpu.VMEM((chan_count, block_size, depth), jnp.bfloat16),
            pltpu.VMEM((chan_count, width, depth), jnp.bfloat16),
            pltpu.VMEM((chan_count, block_size, LANES), jnp.float32),
            pltpu.VMEM((chan_count, 1, width), jnp.float32),
            pltpu.VMEM((slots, block_size, 2 * width), jnp.bfloat16),
            pltpu.SemaphoreType.DMA((chan_count, count + len(chosen) + 1)),
            pltpu.SemaphoreType.DMA,
            pltpu.SemaphoreType.DMA((slots, 2)),
        ],
        input_output_aliases=aliases,
        compiler_params=pltpu.CompilerParams(vmem_limit_bytes=VMEM_LIMIT),
        cost_estimate=pl.CostEstimate(
            flops=4 * chan_count * block_size * width * depth,
            bytes_accessed=4 * chan_count * block_size * (width + depth),
            transcendentals=0,
        ),
    )(places, *operands)


def per_device(voltages, auto_prev, station_order):
    rows, cols = lax.axis_size("row"), lax.axis_size("col")
    row, col = lax.axis_index("row"), lax.axis_index("col")
    height, all_channels, parts, samples = voltages.shape
    chan_count = all_channels // rows
    block_size = height * rows
    offsets = cols // 2 + 1

    def partner_row(turn, parity):
        even, odd = rows_distance(turn, 0, rows), rows_distance(turn, 1, rows)
        return (row ^ jnp.where(parity == 1, odd, even)).astype(jnp.int32)

    autos = [auto_prev]
    for distance in range(2, cols, 2):
        autos.append(swap_with(auto_prev, "col", distance))
    autos = jnp.concatenate(autos, axis=1)
    autos = jnp.concatenate([autos, swap_with(autos, "col", 1)], axis=1)
    own = []
    for turn in range(rows):
        own.append(piece_of(voltages, partner_row(turn, col % 2)[None], chan_count))
        if turn > 0:
            own[turn] = traded(own[turn], turn)

    places_of = [[partner_row(turn, parity) for turn in range(rows)] for parity in (col % 2, 1 - col % 2)]

    split = height % LANES == 0
    if not split:
        stacked = jnp.take(jnp.stack(own, axis=1), jnp.argsort(jnp.stack(places_of[0])), axis=1)
        own = [stacked.reshape(chan_count, block_size, parts * samples)]
    partners = [own]
    for _ in range(1, offsets):
        partners.append([])
        for piece in partners[-2]:
            partners[-1].append(from_behind(piece, "col"))

    first = (col - (offsets - 1)) % cols * block_size
    order = jnp.concatenate([station_order, station_order])
    order = lax.dynamic_slice_in_dim(order, first, offsets * block_size, 0)
    distance = (order // block_size) ^ col
    slot = distance // 2 + distance % 2 * (cols // 2)
    chosen = jnp.take(autos, slot * block_size + order % block_size, axis=1, mode="clip")
    inverse = 1.0 / jnp.sqrt(chosen)
    row_scale = inverse[:, (offsets - 1) * block_size :] * (1.0 / samples)
    row_scale = jnp.broadcast_to(row_scale[:, :, None], (chan_count, block_size, LANES))
    column_scale = inverse[:, None, :]

    shape = (chan_count, offsets, block_size, 2 * block_size)
    count = len(own)
    if split:
        places = [jnp.stack(places_of[0] + partner) for partner in places_of]
    else:
        places = [jnp.zeros((2,), jnp.int32)] * 2
    every, last = list(range(count)), offsets - 1
    tiles = [(offset, every) for offset in range(last)]
    tiles += [(last, [piece]) for piece in every]
    if count > 2:
        tiles = tiles[: last - 1] + tiles[last : last + 2] + [tiles[last - 1]] + tiles[last + 2 :]
    out = None
    for offset, pieces in tiles:
        out = tile_call(
            out,
            shape,
            places[offset % 2],
            own,
            partners[offset],
            row_scale,
            column_scale,
            offset,
            pieces,
        )
    return out


def solution(mesh):
    return jax.shard_map(
        per_device,
        mesh=mesh,
        in_specs=(P(("col", "row"), None, None, None), P("row", "col"), P()),
        out_specs=P("row", None, "col", None),
        check_vma=False,
    )
```

profile of v0, /device:TPU:0, one launch (start us, length us, event | category | flops | bytes accessed | tf_op | source)
XLA Modules:
  0.0 221.4 jit_solution(12497460099350398460)
XLA Ops:
  0.0 2.5 %shard_map.38 = bf16[8,128,512]{2,1,0:T(8,128)(2,1)} custom-call(s32[1]{0:T(128)} %bitcast.1.group_ref, bf16[128,32,2,256]{3,2,1,0:T(2,128)(2,1)} %voltages_ref.7), custom_call_target="tpu_custom_call" | custom-call | tf_op jit(solution)/shard_map/pallas_call | solution.py:49
  2.5 3.0 %collective-permute-start = (bf16[8,128,512]{2,1,0:T(8,128)(2,1)}, bf16[8,128,512]{2,1,0:T(8,128)(2,1)S(1)}, u32[]{:S(2)}, u32[]{:S(2)}) collective-permute-start(bf16[8,128,512]{2,1,0:T(8,128)(2,1)} %shard_map.38), channel_id=1, source_target_pairs={{0,8},{1,17},{2,10},{3,19},{4,12},{5,21},{6,14},{7,23},{8,0},{9,25... | collective-permute-start | bytes 3145736 | tf_op jit(solution)/shard_map/ppermute | solution.py:36
  9.4 2.5 %shard_map.40 = bf16[8,128,512]{2,1,0:T(8,128)(2,1)} custom-call(s32[1]{0:T(128)} %bitcast.3.group_ref, bf16[128,32,2,256]{3,2,1,0:T(2,128)(2,1)} %voltages_ref.7), custom_call_target="tpu_custom_call" | custom-call | tf_op jit(solution)/shard_map/pallas_call | solution.py:49
  11.9 2.5 %shard_map.37.refs_1_.refs_5_ = bf16[8,128,512]{2,1,0:T(8,128)(2,1)} custom-call(s32[1]{0:T(128)} %bitcast.group_ref, bf16[128,32,2,256]{3,2,1,0:T(2,128)(2,1)} %voltages_ref.7), custom_call_target="tpu_custom_call" | custom-call | tf_op jit(solution)/shard_map/pallas_call | solution.py:49
  14.3 12.4 %collective-permute-done.refs_2_.refs_6_ = bf16[8,128,512]{2,1,0:T(8,128)(2,1)S(1)} collective-permute-done((bf16[8,128,512]{2,1,0:T(8,128)(2,1)}, bf16[8,128,512]{2,1,0:T(8,128)(2,1)S(1)}, u32[]{:S(2)}, u32[]{:S(2)}) %collective-permute-start) | collective-permute-done | bytes 1048608 | tf_op jit(solution)/shard_map/ppermute | solution.py:36
  27.7 2.9 %collective-permute-done.1.refs_3_.refs_7_ = bf16[8,128,512]{2,1,0:T(8,128)(2,1)S(1)} collective-permute-done((bf16[8,128,512]{2,1,0:T(8,128)(2,1)}, bf16[8,128,512]{2,1,0:T(8,128)(2,1)S(1)}, u32[]{:S(2)}, u32[]{:S(2)}) %collective-permute-start.1) | collective-permute-done | bytes 1048608 | tf_op jit(solution)/shard_map/ppermute | solution.py:36
  32.9 19.3 %collective-permute-done.2.refs_4_.refs_8_ = bf16[8,128,512]{2,1,0:T(8,128)(2,1)S(1)} collective-permute-done((bf16[8,128,512]{2,1,0:T(8,128)(2,1)}, bf16[8,128,512]{2,1,0:T(8,128)(2,1)S(1)}, u32[]{:S(2)}, u32[]{:S(2)}) %collective-permute-start.2) | collective-permute-done | bytes 1048608 | tf_op jit(solution)/shard_map/ppermute | solution.py:36
  56.8 12.6 %collective-permute-done.3.refs_8_ = bf16[8,128,512]{2,1,0:T(8,128)(2,1)} collective-permute-done((bf16[8,128,512]{2,1,0:T(8,128)(2,1)S(1)}, bf16[8,128,512]{2,1,0:T(8,128)(2,1)}, u32[]{:S(2)}, u32[]{:S(2)}) %collective-permute-start.3) | collective-permute-done | bytes 1048608 | tf_op jit(solution)/shard_map/ppermute | solution.py:20
  70.1 3.3 %collective-permute-done.7 = f32[8,512]{1,0:T(8,128)S(1)} collective-permute-done((f32[8,512]{1,0:T(8,128)}, f32[8,512]{1,0:T(8,128)S(1)}, u32[]{:S(2)}, u32[]{:S(2)}) %collective-permute-start.7) | collective-permute-done | bytes 16416 | tf_op jit(solution)/shard_map/ppermute | solution.py:15
  74.2 17.9 %collective-permute-done.8 = f32[8,512]{1,0:T(8,128)S(1)} collective-permute-done((f32[8,512]{1,0:T(8,128)}, f32[8,512]{1,0:T(8,128)S(1)}, u32[]{:S(2)}, u32[]{:S(2)}) %collective-permute-start.8) | collective-permute-done | bytes 16416 | tf_op jit(solution)/shard_map/ppermute | solution.py:15
  93.3 4.7 %collective-permute-done.9 = f32[8,512]{1,0:T(8,128)S(1)} collective-permute-done((f32[8,512]{1,0:T(8,128)}, f32[8,512]{1,0:T(8,128)S(1)}, u32[]{:S(2)}, u32[]{:S(2)}) %collective-permute-start.9) | collective-permute-done | bytes 16416 | tf_op jit(solution)/shard_map/ppermute | solution.py:15
  98.8 21.7 %collective-permute-start.10 = (f32[8,2048]{1,0:T(8,128)S(1)}, f32[8,2048]{1,0:T(8,128)S(1)}, u32[]{:S(2)}, u32[]{:S(2)}) collective-permute-start(f32[8,2048]{1,0:T(8,128)S(1)} %pad_maximum_fusion), channel_id=1, source_target_pairs={{0,1},{1,0},{2,3},{3,2},{4,5},{5,4},{6,7},{7,6},{8,9},{9,8},{10,11... | collective-permute-start | bytes 196616 | tf_op jit(solution)/shard_map/ppermute | solution.py:15
  121.9 4.2 %gather_fusion = f32[2560,8]{1,0:T(8,128)S(1)} fusion(f32[8,4096]{0,1:T(8,128)S(1)} %copy.17, s32[3072]{0:T(1024)S(1)} %pad_clamp_fusion), kind=kCustom, calls=%fused_computation | custom fusion | bytes 174080 | tf_op jit(solution)/shard_map/jit(_take)/gather | solution.py:247
  127.6 9.2 %collective-permute-done.17.refs_5_ = bf16[8,128,512]{2,1,0:T(8,128)(2,1)} collective-permute-done((bf16[8,128,512]{2,1,0:T(8,128)(2,1)}, bf16[8,128,512]{2,1,0:T(8,128)(2,1)}, u32[]{:S(2)}, u32[]{:S(2)}) %collective-permute-start.17) | collective-permute-done | bytes 1048608 | tf_op jit(solution)/shard_map/ppermute | solution.py:20
  136.8 11.2 %collective-permute-done.20.refs_6_ = bf16[8,128,512]{2,1,0:T(8,128)(2,1)} collective-permute-done((bf16[8,128,512]{2,1,0:T(8,128)(2,1)}, bf16[8,128,512]{2,1,0:T(8,128)(2,1)}, u32[]{:S(2)}, u32[]{:S(2)}) %collective-permute-start.20) | collective-permute-done | bytes 1048608 | tf_op jit(solution)/shard_map/ppermute | solution.py:20
  150.0 11.0 %shard_map.41.refs_11_ = bf16[8,5,512,1024]{3,2,1,0:T(8,128)(2,1)} custom-call(s32[8]{0:T(128)} %stack.38.refs_0_, bf16[8,128,512]{2,1,0:T(8,128)(2,1)} %shard_map.37.refs_1_.refs_5_, bf16[8,128,512]{2,1,0:T(8,128)(2,1)} %copy-done, bf16[8,128,512]{2,1,0:T(8,128)(2,1)} %copy-done.1, bf16[8,128,512]{2,1,0:T(8,128)(2,1)} %copy-done.2, ...), custom_call_target="tpu_custom_call" | custom-call | flops 4294967296 | bytes 16777216 | tf_op jit(solution)/shard_map/pallas_call | solution.py:182
  161.1 10.4 %shard_map.42.refs_11_ = bf16[8,5,512,1024]{3,2,1,0:T(8,128)(2,1)} custom-call(s32[8]{0:T(128)} %stack.41.refs_0_, bf16[8,128,512]{2,1,0:T(8,128)(2,1)} %shard_map.37.refs_1_.refs_5_, bf16[8,128,512]{2,1,0:T(8,128)(2,1)} %copy-done, bf16[8,128,512]{2,1,0:T(8,128)(2,1)} %copy-done.1, bf16[8,128,512]{2,1,0:T(8,128)(2,1)} %copy-done.2, ...), custom_call_target="tpu_custom_call", output_to_operand_aliasing={{}: (11, {})} | custom-call | flops 4294967296 | bytes 16777216 | tf_op jit(solution)/shard_map/pallas_call | solution.py:182
  171.6 10.4 %shard_map.43.refs_8_ = bf16[8,5,512,1024]{3,2,1,0:T(8,128)(2,1)} custom-call(s32[8]{0:T(128)} %stack.38.refs_0_, bf16[8,128,512]{2,1,0:T(8,128)(2,1)} %shard_map.37.refs_1_.refs_5_, bf16[8,128,512]{2,1,0:T(8,128)(2,1)} %copy-done, bf16[8,128,512]{2,1,0:T(8,128)(2,1)} %copy-done.1, bf16[8,128,512]{2,1,0:T(8,128)(2,1)} %copy-done.2, ...), custom_call_target="tpu_custom_call", output_to_operand_aliasing={{}: (11, {})} | custom-call | flops 4294967296 | bytes 16777216 | tf_op jit(solution)/shard_map/pallas_call | solution.py:182
  182.0 6.0 %shard_map.44.refs_8_ = bf16[8,5,512,1024]{3,2,1,0:T(8,128)(2,1)} custom-call(s32[8]{0:T(128)} %stack.38.refs_0_, bf16[8,128,512]{2,1,0:T(8,128)(2,1)} %shard_map.37.refs_1_.refs_5_, bf16[8,128,512]{2,1,0:T(8,128)(2,1)} %copy-done, bf16[8,128,512]{2,1,0:T(8,128)(2,1)} %copy-done.1, bf16[8,128,512]{2,1,0:T(8,128)(2,1)} %copy-done.2, ...), custom_call_target="tpu_custom_call", output_to_operand_aliasing={{}: (8, {})} | custom-call | flops 1073741824 | bytes 10485760 | tf_op jit(solution)/shard_map/pallas_call | solution.py:182
  188.0 5.1 %collective-permute-done.21.refs_5_ = bf16[8,128,512]{2,1,0:T(8,128)(2,1)} collective-permute-done((bf16[8,128,512]{2,1,0:T(8,128)(2,1)}, bf16[8,128,512]{2,1,0:T(8,128)(2,1)}, u32[]{:S(2)}, u32[]{:S(2)}) %collective-permute-start.21) | collective-permute-done | bytes 1048608 | tf_op jit(solution)/shard_map/ppermute | solution.py:20
  193.0 6.0 %shard_map.45.refs_11_ = bf16[8,5,512,1024]{3,2,1,0:T(8,128)(2,1)} custom-call(s32[8]{0:T(128)} %stack.38.refs_0_, bf16[8,128,512]{2,1,0:T(8,128)(2,1)} %shard_map.37.refs_1_.refs_5_, bf16[8,128,512]{2,1,0:T(8,128)(2,1)} %copy-done, bf16[8,128,512]{2,1,0:T(8,128)(2,1)} %copy-done.1, bf16[8,128,512]{2,1,0:T(8,128)(2,1)} %copy-done.2, ...), custom_call_target="tpu_custom_call", output_to_operand_aliasing={{}: (8, {})} | custom-call | flops 1073741824 | bytes 10485760 | tf_op jit(solution)/shard_map/pallas_call | solution.py:182
  199.0 10.4 %shard_map.46.refs_8_ = bf16[8,5,512,1024]{3,2,1,0:T(8,128)(2,1)} custom-call(s32[8]{0:T(128)} %stack.41.refs_0_, bf16[8,128,512]{2,1,0:T(8,128)(2,1)} %shard_map.37.refs_1_.refs_5_, bf16[8,128,512]{2,1,0:T(8,128)(2,1)} %copy-done, bf16[8,128,512]{2,1,0:T(8,128)(2,1)} %copy-done.1, bf16[8,128,512]{2,1,0:T(8,128)(2,1)} %copy-done.2, ...), custom_call_target="tpu_custom_call", output_to_operand_aliasing={{}: (11, {})} | custom-call | flops 4294967296 | bytes 16777216 | tf_op jit(solution)/shard_map/pallas_call | solution.py:182
  209.4 6.0 %shard_map.47.refs_8_ = bf16[8,5,512,1024]{3,2,1,0:T(8,128)(2,1)} custom-call(s32[8]{0:T(128)} %stack.38.refs_0_, bf16[8,128,512]{2,1,0:T(8,128)(2,1)} %shard_map.37.refs_1_.refs_5_, bf16[8,128,512]{2,1,0:T(8,128)(2,1)} %copy-done, bf16[8,128,512]{2,1,0:T(8,128)(2,1)} %copy-done.1, bf16[8,128,512]{2,1,0:T(8,128)(2,1)} %copy-done.2, ...), custom_call_target="tpu_custom_call", output_to_operand_aliasing={{}: (8, {})} | custom-call | flops 1073741824 | bytes 10485760 | tf_op jit(solution)/shard_map/pallas_call | solution.py:182
  215.5 6.0 %shard_map.48 = bf16[8,5,512,1024]{3,2,1,0:T(8,128)(2,1)} custom-call(s32[8]{0:T(128)} %stack.38.refs_0_, bf16[8,128,512]{2,1,0:T(8,128)(2,1)} %shard_map.37.refs_1_.refs_5_, bf16[8,128,512]{2,1,0:T(8,128)(2,1)} %copy-done, bf16[8,128,512]{2,1,0:T(8,128)(2,1)} %copy-done.1, bf16[8,128,512]{2,1,0:T(8,128)(2,1)} %copy-done.2, ...), custom_call_target="tpu_custom_call", output_to_operand_aliasing={{}: (8, {})} | custom-call | flops 1073741824 | bytes 10485760 | tf_op jit(solution)/shard_map/pallas_call | solution.py:182
  (57 shorter events, 20.5 us)
Async XLA Ops:
  2.5 24.3 %collective-permute-start = (bf16[8,128,512]{2,1,0:T(8,128)(2,1)}, bf16[8,128,512]{2,1,0:T(8,128)(2,1)S(1)}, u32[]{:S(2)}, u32[]{:S(2)}) collective-permute-start(bf16[8,128,512]{2,1,0:T(8,128)(2,1)} %shard_map.38), channel_id=1, source_target_pairs={{0,8},{1,17},{2,10},{3,19},{4,12},{5,21},{6,14},{7,23},{8,0},{9,25... | collective-permute-start | bytes 3145736 | tf_op jit(solution)/shard_map/ppermute | solution.py:36
  7.9 22.7 %collective-permute-start.1 = (bf16[8,128,512]{2,1,0:T(8,128)(2,1)}, bf16[8,128,512]{2,1,0:T(8,128)(2,1)S(1)}, u32[]{:S(2)}, u32[]{:S(2)}) collective-permute-start(bf16[8,128,512]{2,1,0:T(8,128)(2,1)} %shard_map.39), channel_id=1, source_target_pairs={{0,16},{1,9},{2,18},{3,11},{4,20},{5,13},{6,22},{7,15},{8,24},{9,1... | collective-permute-start | bytes 3145736 | tf_op jit(solution)/shard_map/ppermute | solution.py:36
  11.8 40.4 %collective-permute-start.2 = (bf16[8,128,512]{2,1,0:T(8,128)(2,1)}, bf16[8,128,512]{2,1,0:T(8,128)(2,1)S(1)}, u32[]{:S(2)}, u32[]{:S(2)}) collective-permute-start(bf16[8,128,512]{2,1,0:T(8,128)(2,1)} %shard_map.40), channel_id=1, source_target_pairs={{0,24},{1,25},{2,26},{3,27},{4,28},{5,29},{6,30},{7,31},{8,16},{9,... | collective-permute-start | bytes 3145736 | tf_op jit(solution)/shard_map/ppermute | solution.py:36
  14.3 39.5 %collective-permute-start.15 = (bf16[8,128,512]{2,1,0:T(8,128)(2,1)}, bf16[8,128,512]{2,1,0:T(8,128)(2,1)}, u32[]{:S(2)}, u32[]{:S(2)}) collective-permute-start(bf16[8,128,512]{2,1,0:T(8,128)(2,1)} %shard_map.37.refs_1_.refs_5_), channel_id=1, source_target_pairs={{0,1},{1,2},{2,3},{3,4},{4,5},{5,6},{6,7},{7,0},{8,9},{9,10},{10,1... | collective-permute-start | bytes 3145736 | tf_op jit(solution)/shard_map/ppermute | solution.py:20
  27.7 26.2 %collective-permute-start.18 = (bf16[8,128,512]{2,1,0:T(8,128)(2,1)S(1)}, bf16[8,128,512]{2,1,0:T(8,128)(2,1)}, u32[]{:S(2)}, u32[]{:S(2)}) collective-permute-start(bf16[8,128,512]{2,1,0:T(8,128)(2,1)S(1)} %collective-permute-done.refs_2_.refs_6_), channel_id=1, source_target_pairs={{0,1},{1,2},{2,3},{3,4},{4,5},{5,6},{6,7},{7,0},{8,9},{9,10},{10,1... | collective-permute-start | bytes 3145736 | tf_op jit(solution)/shard_map/ppermute | solution.py:20
  30.6 23.3 %copy-start.1 = (bf16[8,128,512]{2,1,0:T(8,128)(2,1)}, bf16[8,128,512]{2,1,0:T(8,128)(2,1)S(1)}, u32[]{:S(2)}) copy-start(bf16[8,128,512]{2,1,0:T(8,128)(2,1)S(1)} %collective-permute-done.1.refs_3_.refs_7_) | copy-start | bytes 3145732
  30.6 26.1 %collective-permute-start.11 = (bf16[8,128,512]{2,1,0:T(8,128)(2,1)S(1)}, bf16[8,128,512]{2,1,0:T(8,128)(2,1)}, u32[]{:S(2)}, u32[]{:S(2)}) collective-permute-start(bf16[8,128,512]{2,1,0:T(8,128)(2,1)S(1)} %collective-permute-done.1.refs_3_.refs_7_), channel_id=1, source_target_pairs={{0,1},{1,2},{2,3},{3,4},{4,5},{5,6},{6,7},{7,0},{8,9},{9,10},{10,1... | collective-permute-start | bytes 3145736 | tf_op jit(solution)/shard_map/ppermute | solution.py:20
  52.3 17.1 %collective-permute-start.3 = (bf16[8,128,512]{2,1,0:T(8,128)(2,1)S(1)}, bf16[8,128,512]{2,1,0:T(8,128)(2,1)}, u32[]{:S(2)}, u32[]{:S(2)}) collective-permute-start(bf16[8,128,512]{2,1,0:T(8,128)(2,1)S(1)} %collective-permute-done.2.refs_4_.refs_8_), channel_id=1, source_target_pairs={{0,1},{1,2},{2,3},{3,4},{4,5},{5,6},{6,7},{7,0},{8,9},{9,10},{10,1... | collective-permute-start | bytes 3145736 | tf_op jit(solution)/shard_map/ppermute | solution.py:20
  53.8 66.6 %collective-permute-start.16 = (bf16[8,128,512]{2,1,0:T(8,128)(2,1)}, bf16[8,128,512]{2,1,0:T(8,128)(2,1)}, u32[]{:S(2)}, u32[]{:S(2)}) collective-permute-start(bf16[8,128,512]{2,1,0:T(8,128)(2,1)} %collective-permute-done.15.refs_5_), channel_id=1, source_target_pairs={{0,1},{1,2},{2,3},{3,4},{4,5},{5,6},{6,7},{7,0},{8,9},{9,10},{10,1... | collective-permute-start | bytes 3145736 | tf_op jit(solution)/shard_map/ppermute | solution.py:20
  53.9 66.6 %collective-permute-start.19 = (bf16[8,128,512]{2,1,0:T(8,128)(2,1)}, bf16[8,128,512]{2,1,0:T(8,128)(2,1)}, u32[]{:S(2)}, u32[]{:S(2)}) collective-permute-start(bf16[8,128,512]{2,1,0:T(8,128)(2,1)} %collective-permute-done.18.refs_6_), channel_id=1, source_target_pairs={{0,1},{1,2},{2,3},{3,4},{4,5},{5,6},{6,7},{7,0},{8,9},{9,10},{10,1... | collective-permute-start | bytes 3145736 | tf_op jit(solution)/shard_map/ppermute | solution.py:20
  55.1 18.3 %collective-permute-start.7 = (f32[8,512]{1,0:T(8,128)}, f32[8,512]{1,0:T(8,128)S(1)}, u32[]{:S(2)}, u32[]{:S(2)}) collective-permute-start(f32[8,512]{1,0:T(8,128)} %param.4), channel_id=1, source_target_pairs={{0,2},{1,3},{2,0},{3,1},{4,6},{5,7},{6,4},{7,5},{8,10},{9,11},{10,... | collective-permute-start | bytes 49160 | tf_op jit(solution)/shard_map/ppermute | solution.py:15
  56.7 69.8 %collective-permute-start.12 = (bf16[8,128,512]{2,1,0:T(8,128)(2,1)}, bf16[8,128,512]{2,1,0:T(8,128)(2,1)}, u32[]{:S(2)}, u32[]{:S(2)}) collective-permute-start(bf16[8,128,512]{2,1,0:T(8,128)(2,1)} %collective-permute-done.11.refs_7_), channel_id=1, source_target_pairs={{0,1},{1,2},{2,3},{3,4},{4,5},{5,6},{6,7},{7,0},{8,9},{9,10},{10,1... | collective-permute-start | bytes 3145736 | tf_op jit(solution)/shard_map/ppermute | solution.py:20
  69.4 57.5 %collective-permute-start.4 = (bf16[8,128,512]{2,1,0:T(8,128)(2,1)}, bf16[8,128,512]{2,1,0:T(8,128)(2,1)}, u32[]{:S(2)}, u32[]{:S(2)}) collective-permute-start(bf16[8,128,512]{2,1,0:T(8,128)(2,1)} %collective-permute-done.3.refs_8_), channel_id=1, source_target_pairs={{0,1},{1,2},{2,3},{3,4},{4,5},{5,6},{6,7},{7,0},{8,9},{9,10},{10,1... | collective-permute-start | bytes 3145736 | tf_op jit(solution)/shard_map/ppermute | solution.py:20
  73.4 18.7 %collective-permute-start.8 = (f32[8,512]{1,0:T(8,128)}, f32[8,512]{1,0:T(8,128)S(1)}, u32[]{:S(2)}, u32[]{:S(2)}) collective-permute-start(f32[8,512]{1,0:T(8,128)} %param.4), channel_id=1, source_target_pairs={{0,4},{1,5},{2,6},{3,7},{4,0},{5,1},{6,2},{7,3},{8,12},{9,13},{10,... | collective-permute-start | bytes 49160 | tf_op jit(solution)/shard_map/ppermute | solution.py:15
  92.1 5.9 %collective-permute-start.9 = (f32[8,512]{1,0:T(8,128)}, f32[8,512]{1,0:T(8,128)S(1)}, u32[]{:S(2)}, u32[]{:S(2)}) collective-permute-start(f32[8,512]{1,0:T(8,128)} %param.4), channel_id=1, source_target_pairs={{0,6},{1,7},{2,4},{3,5},{4,2},{5,3},{6,0},{7,1},{8,14},{9,15},{10,... | collective-permute-start | bytes 49160 | tf_op jit(solution)/shard_map/ppermute | solution.py:15
  98.8 22.6 %collective-permute-start.10 = (f32[8,2048]{1,0:T(8,128)S(1)}, f32[8,2048]{1,0:T(8,128)S(1)}, u32[]{:S(2)}, u32[]{:S(2)}) collective-permute-start(f32[8,2048]{1,0:T(8,128)S(1)} %pad_maximum_fusion), channel_id=1, source_target_pairs={{0,1},{1,0},{2,3},{3,2},{4,5},{5,4},{6,7},{7,6},{8,9},{9,8},{10,11... | collective-permute-start | bytes 196616 | tf_op jit(solution)/shard_map/ppermute | solution.py:15
  120.4 16.4 %collective-permute-start.17 = (bf16[8,128,512]{2,1,0:T(8,128)(2,1)}, bf16[8,128,512]{2,1,0:T(8,128)(2,1)}, u32[]{:S(2)}, u32[]{:S(2)}) collective-permute-start(bf16[8,128,512]{2,1,0:T(8,128)(2,1)} %collective-permute-done.16.refs_5_), channel_id=1, source_target_pairs={{0,1},{1,2},{2,3},{3,4},{4,5},{5,6},{6,7},{7,0},{8,9},{9,10},{10,1... | collective-permute-start | bytes 3145736 | tf_op jit(solution)/shard_map/ppermute | solution.py:20
  120.5 27.5 %collective-permute-start.20 = (bf16[8,128,512]{2,1,0:T(8,128)(2,1)}, bf16[8,128,512]{2,1,0:T(8,128)(2,1)}, u32[]{:S(2)}, u32[]{:S(2)}) collective-permute-start(bf16[8,128,512]{2,1,0:T(8,128)(2,1)} %collective-permute-done.19.refs_6_), channel_id=1, source_target_pairs={{0,1},{1,2},{2,3},{3,4},{4,5},{5,6},{6,7},{7,0},{8,9},{9,10},{10,1... | collective-permute-start | bytes 3145736 | tf_op jit(solution)/shard_map/ppermute | solution.py:20
  126.5 34.6 %collective-permute-start.13 = (bf16[8,128,512]{2,1,0:T(8,128)(2,1)}, bf16[8,128,512]{2,1,0:T(8,128)(2,1)}, u32[]{:S(2)}, u32[]{:S(2)}) collective-permute-start(bf16[8,128,512]{2,1,0:T(8,128)(2,1)} %collective-permute-done.12.refs_7_), channel_id=1, source_target_pairs={{0,1},{1,2},{2,3},{3,4},{4,5},{5,6},{6,7},{7,0},{8,9},{9,10},{10,1... | collective-permute-start | bytes 3145736 | tf_op jit(solution)/shard_map/ppermute | solution.py:20
  126.9 44.7 %collective-permute-start.5 = (bf16[8,128,512]{2,1,0:T(8,128)(2,1)}, bf16[8,128,512]{2,1,0:T(8,128)(2,1)}, u32[]{:S(2)}, u32[]{:S(2)}) collective-permute-start(bf16[8,128,512]{2,1,0:T(8,128)(2,1)} %collective-permute-done.4.refs_8_), channel_id=1, source_target_pairs={{0,1},{1,2},{2,3},{3,4},{4,5},{5,6},{6,7},{7,0},{8,9},{9,10},{10,1... | collective-permute-start | bytes 3145736 | tf_op jit(solution)/shard_map/ppermute | solution.py:20
  136.8 45.1 %collective-permute-start.22 = (bf16[8,128,512]{2,1,0:T(8,128)(2,1)}, bf16[8,128,512]{2,1,0:T(8,128)(2,1)}, u32[]{:S(2)}, u32[]{:S(2)}) collective-permute-start(bf16[8,128,512]{2,1,0:T(8,128)(2,1)} %collective-permute-done.17.refs_5_), channel_id=1, source_target_pairs={{0,1},{1,2},{2,3},{3,4},{4,5},{5,6},{6,7},{7,0},{8,9},{9,10},{10,1... | collective-permute-start | bytes 3145736 | tf_op jit(solution)/shard_map/ppermute | solution.py:20
  148.1 44.9 %collective-permute-start.21 = (bf16[8,128,512]{2,1,0:T(8,128)(2,1)}, bf16[8,128,512]{2,1,0:T(8,128)(2,1)}, u32[]{:S(2)}, u32[]{:S(2)}) collective-permute-start(bf16[8,128,512]{2,1,0:T(8,128)(2,1)} %collective-permute-done.20.refs_6_), channel_id=1, source_target_pairs={{0,1},{1,2},{2,3},{3,4},{4,5},{5,6},{6,7},{7,0},{8,9},{9,10},{10,1... | collective-permute-start | bytes 3145736 | tf_op jit(solution)/shard_map/ppermute | solution.py:20
  161.1 48.3 %collective-permute-start.14 = (bf16[8,128,512]{2,1,0:T(8,128)(2,1)}, bf16[8,128,512]{2,1,0:T(8,128)(2,1)}, u32[]{:S(2)}, u32[]{:S(2)}) collective-permute-start(bf16[8,128,512]{2,1,0:T(8,128)(2,1)} %collective-permute-done.13.refs_7_), channel_id=1, source_target_pairs={{0,1},{1,2},{2,3},{3,4},{4,5},{5,6},{6,7},{7,0},{8,9},{9,10},{10,1... | collective-permute-start | bytes 3145736 | tf_op jit(solution)/shard_map/ppermute | solution.py:20
  171.5 43.9 %collective-permute-start.6 = (bf16[8,128,512]{2,1,0:T(8,128)(2,1)}, bf16[8,128,512]{2,1,0:T(8,128)(2,1)}, u32[]{:S(2)}, u32[]{:S(2)}) collective-permute-start(bf16[8,128,512]{2,1,0:T(8,128)(2,1)} %collective-permute-done.5.refs_8_), channel_id=1, source_target_pairs={{0,1},{1,2},{2,3},{3,4},{4,5},{5,6},{6,7},{7,0},{8,9},{9,10},{10,1... | collective-permute-start | bytes 3145736 | tf_op jit(solution)/shard_map/ppermute | solution.py:20
  (2 other events, 5.4 us)
where the time goes:
time: 222 us; the launch traced here: 221 us
  waiting for transfers between devices  99.5 us (45%)
  Pallas kernels  75.8 us (34%)
  starting transfers between devices  33.7 us (15%)
  local copies, waits for them, and re-layouts  10.7 us (5%)
    pallas_call x8, Pallas kernels, tile_call(): pl.pallas_call(body, in_specs=in_specs, out_specs=pl.BlockSpec(memory_spa...  66 us
    ppermute x16, waiting for transfers between devices, from_behind(): lax.ppermute(value, axis, [(i, (i + 1) % count) for i in range(count)])  38.3 us
    ppermute x3, waiting for transfers between devices, traded(): return lax.ppermute(value, ('row', 'col'), pairs)  34.6 us
    ppermute x4, waiting for transfers between devices, swap_with(): return lax.ppermute(value, axis, [(i, i ^ distance) for i in range(count)])  26.6 us
    ppermute x4, starting transfers between devices, swap_with(): return lax.ppermute(value, axis, [(i, i ^ distance) for i in range(count)])  23.3 us
    pallas_call x4, Pallas kernels, piece_of(): pl.pallas_call(gather_piece, grid_spec=pltpu.PrefetchScalarGridSpec(num_s...  9.82 us
    ppermute x16, starting transfers between devices, from_behind(): lax.ppermute(value, axis, [(i, (i + 1) % count) for i in range(count)])  6 us
    gather x2, local copies, waits for them, and re-layouts, per_device(): jnp.take(autos, slot * block_size + order % block_size, axis=1, mode='clip')  4.51 us
  transfers between devices with their start and end apart: 23, of which 12 were waited for; matrix products, arithmetic and copies ran while one was open for 5% of the time, Pallas kernels for 30%

commit v1 on v0

--- a/solution.py
+++ b/solution.py
@@ -7,7 +7,7 @@
 
 
 LANES = 128
-VMEM_LIMIT = 253 * 256 * 1024
+VMEM_LIMIT = 255 * 256 * 1024
 
 
 def swap_with(value, axis, distance):
@@ -71,11 +71,11 @@
     )
 
 
-def tiles_kernel(count, chosen, offset, column_start, slots, places_ref, *refs):
+def tiles_kernel(count, chosen, offset, column_start, base, slots, places_ref, *refs):
     own, partner = refs[:count], refs[count : count + len(chosen)]
     row_scale_ref, column_scale_ref = refs[count + len(chosen) : count + len(chosen) + 2]
     out_ref, left_ref, right_ref, rows_ref, columns_ref, stage_ref, loaded, read, sent = refs[-9:]
-    chan_count, height, _ = own[0].shape
+    chan_count, height, _ = partner[0].shape
     block_size = height * count
     whole = len(chosen) == count
     width = height * len(chosen)
@@ -90,8 +90,9 @@
             top = 0
             if index < count or whole:
                 top = pl.multiple_of(places_ref[index] * height, height)
-            result.append((ref.at[chan], to_ref.at[chan, pl.ds(top, height)]))
-        result.append((row_scale_ref.at[chan], rows_ref.at[chan]))
+            source = ref.at[base + chan] if index < count else ref.at[chan]
+            result.append((source, to_ref.at[chan, pl.ds(top, height)]))
+        result.append((row_scale_ref.at[base + chan], rows_ref.at[chan]))
         return [
             pltpu.make_async_copy(source, target, loaded.at[chan, index])
             for index, (source, target) in enumerate(result)
@@ -100,7 +101,7 @@
     def sends(chan):
         slot = chan % slots
         if whole:
-            return [pltpu.make_async_copy(stage_ref.at[slot], out_ref.at[chan, offset], sent.at[slot, 0])]
+            return [pltpu.make_async_copy(stage_ref.at[slot], out_ref.at[base + chan, offset], sent.at[slot, 0])]
         result = []
         for part in range(2):
             column = part * block_size + places_ref[count + chosen[0]] * height
@@ -108,14 +109,14 @@
             result.append(
                 pltpu.make_async_copy(
                     stage_ref.at[slot, :, pl.ds(part * height, height)],
-                    out_ref.at[chan, offset, :, pl.ds(column, height)],
+                    out_ref.at[base + chan, offset, :, pl.ds(column, height)],
                     sent.at[slot, part],
                 )
             )
         return result
 
     columns_load = pltpu.make_async_copy(
-        column_scale_ref.at[:, :, pl.ds(first_column, width)], columns_ref, read
+        column_scale_ref.at[pl.ds(base, chan_count), :, pl.ds(first_column, width)], columns_ref, read
     )
     columns_load.start()
 
@@ -162,12 +163,12 @@
     lax.fori_loop(chan_count - slots, chan_count, drain, 0)
 
 
-def tile_call(out, shape, places, own, partner, row_scale, column_scale, offset, chosen):
-    chan_count, offsets, block_size, _ = shape
-    count, (_, height, depth) = len(own), own[0].shape
+def tile_call(out, shape, places, own, partner, row_scale, column_scale, offset, chosen, base=0):
+    _, offsets, block_size, _ = shape
+    count, (chan_count, height, depth) = len(own), partner[0].shape
     slots = 2 if len(chosen) == count else chan_count
     width = height * len(chosen)
-    operands = [*own, *[partner[piece] for piece in chosen], row_scale, column_scale]
+    operands = [*own, *partner, row_scale, column_scale]
     aliases = {}
     if out is not None:
         aliases = {1 + len(operands): 0}
@@ -177,7 +178,7 @@
     column_start = (offsets - 1 - offset) * block_size
 
     def body(*refs):
-        tiles_kernel(count, chosen, offset, column_start, slots, *refs)
+        tiles_kernel(count, chosen, offset, column_start, base, slots, *refs)
 
     return pl.pallas_call(
         body,
@@ -234,9 +235,16 @@
         stacked = jnp.take(jnp.stack(own, axis=1), jnp.argsort(jnp.stack(places_of[0])), axis=1)
         own = [stacked.reshape(chan_count, block_size, parts * samples)]
     partners = [own]
-    for _ in range(1, offsets):
+    for offset in range(1, offsets):
         partners.append([])
-        for piece in partners[-2]:
+        for index, piece in enumerate(partners[-2]):
+            if split and offset == offsets - 1 and index == len(own) - 1:
+                half = chan_count // 2
+                lower, upper = piece[:half], piece[half:]
+                lower = from_behind(lower, "col")
+                upper = from_behind(upper, "col")
+                partners[-1].append([lower, upper])
+                continue
             partners[-1].append(from_behind(piece, "col"))
 
     first = (col - (offsets - 1)) % cols * block_size
@@ -263,17 +271,22 @@
         tiles = tiles[: last - 1] + tiles[last : last + 2] + [tiles[last - 1]] + tiles[last + 2 :]
     out = None
     for offset, pieces in tiles:
-        out = tile_call(
-            out,
-            shape,
-            places[offset % 2],
-            own,
-            partners[offset],
-            row_scale,
-            column_scale,
-            offset,
-            pieces,
-        )
+        base = 0
+        partner = [partners[offset][piece] for piece in pieces]
+        for part in partner[0] if isinstance(partner[0], list) else [None]:
+            out = tile_call(
+                out,
+                shape,
+                places[offset % 2],
+                own,
+                partner if part is None else [part],
+                row_scale,
+                column_scale,
+                offset,
+                pieces,
+                base,
+            )
+            base += 0 if part is None else part.shape[0]
     return out
 
 

time: 222 us -> 235 us (1.059)
  starting transfers between devices: 33.7 us -> 59.1 us
  waiting for transfers between devices: 99.5 us -> 82.4 us
  Pallas kernels: 75.8 us -> 78.3 us
    ppermute x3, waiting for transfers between devices: 34.6 us -> 19.4 us  [traded(): return lax.ppermute(value, ('row', 'col'), pairs)]
    ppermute x16 -> x17, starting transfers between devices: 6 us -> 19.9 us  [from_behind(): lax.ppermute(value, axis, [(i, (i + 1) % count) for i in range(count)])]
    ppermute x4, starting transfers between devices: 23.3 us -> 34.7 us  [swap_with(): return lax.ppermute(value, axis, [(i, i ^ distance) for i in range(count)])]
    ppermute x4, waiting for transfers between devices: 26.6 us -> 15.5 us  [swap_with(): return lax.ppermute(value, axis, [(i, i ^ distance) for i in range(count)])]
    ppermute x16 -> x17, waiting for transfers between devices: 38.3 us -> 47.5 us  [from_behind(): lax.ppermute(value, axis, [(i, (i + 1) % count) for i in range(count)])]
    pallas_call x8 -> x9, Pallas kernels: 66 us -> 68.5 us  [tile_call(): pl.pallas_call(body, in_specs=in_specs, out_specs=pl.BlockSpec(memory_spa...]
  transfers between devices with their start and end apart: 23 -> 24, of which waited for: 12 -> 13; matrix products, arithmetic and copies ran while one was open for 5% -> 6% of each run, Pallas kernels for 30% -> 31%
where the time goes in v1:
time: 235 us; the launch traced here: 234 us
  waiting for transfers between devices  82.4 us (35%)
  Pallas kernels  78.3 us (33%)
  starting transfers between devices  59.1 us (25%)
  local copies, waits for them, and re-layouts  12.9 us (5%)
    pallas_call x9, Pallas kernels, tile_call(): pl.pallas_call(body, in_specs=in_specs, out_specs=pl.BlockSpec(memory_spa...  68.5 us
    ppermute x17, waiting for transfers between devices, from_behind(): lax.ppermute(value, axis, [(i, (i + 1) % count) for i in range(count)])  47.5 us
    ppermute x4, starting transfers between devices, swap_with(): return lax.ppermute(value, axis, [(i, i ^ distance) for i in range(count)])  34.7 us
    ppermute x17, starting transfers between devices, from_behind(): lax.ppermute(value, axis, [(i, (i + 1) % count) for i in range(count)])  19.9 us
    ppermute x3, waiting for transfers between devices, traded(): return lax.ppermute(value, ('row', 'col'), pairs)  19.4 us
    ppermute x4, waiting for transfers between devices, swap_with(): return lax.ppermute(value, axis, [(i, i ^ distance) for i in range(count)])  15.5 us
    pallas_call x4, Pallas kernels, piece_of(): pl.pallas_call(gather_piece, grid_spec=pltpu.PrefetchScalarGridSpec(num_s...  9.83 us
  transfers between devices with their start and end apart: 24, of which 13 were waited for; matrix products, arithmetic and copies ran while one was open for 6% of the time, Pallas kernels for 31%

profile of v1, /device:TPU:0, one launch (start us, length us, event | category | flops | bytes accessed | tf_op | source)
XLA Modules:
  0.0 234.4 jit_solution(18295290435315959250)
XLA Ops:
  0.0 2.5 %shard_map.39 = bf16[8,128,512]{2,1,0:T(8,128)(2,1)} custom-call(s32[1]{0:T(128)} %bitcast.2.group_ref, bf16[128,32,2,256]{3,2,1,0:T(2,128)(2,1)} %voltages_ref.7), custom_call_target="tpu_custom_call" | custom-call | tf_op jit(solution)/shard_map/pallas_call | solution.py:49
  2.5 3.0 %collective-permute-start.1 = (bf16[8,128,512]{2,1,0:T(8,128)(2,1)}, bf16[8,128,512]{2,1,0:T(8,128)(2,1)S(1)}, u32[]{:S(2)}, u32[]{:S(2)}) collective-permute-start(bf16[8,128,512]{2,1,0:T(8,128)(2,1)} %shard_map.39), channel_id=1, source_target_pairs={{0,16},{1,9},{2,18},{3,11},{4,20},{5,13},{6,22},{7,15},{8,24},{9,1... | collective-permute-start | bytes 3145736 | tf_op jit(solution)/shard_map/ppermute | solution.py:36
  11.9 2.5 %shard_map.37.refs_1_.refs_5_ = bf16[8,128,512]{2,1,0:T(8,128)(2,1)} custom-call(s32[1]{0:T(128)} %bitcast.group_ref, bf16[128,32,2,256]{3,2,1,0:T(2,128)(2,1)} %voltages_ref.7), custom_call_target="tpu_custom_call" | custom-call | tf_op jit(solution)/shard_map/pallas_call | solution.py:49
  14.3 16.2 %collective-permute-done.1.refs_3_.refs_7_ = bf16[8,128,512]{2,1,0:T(8,128)(2,1)S(1)} collective-permute-done((bf16[8,128,512]{2,1,0:T(8,128)(2,1)}, bf16[8,128,512]{2,1,0:T(8,128)(2,1)S(1)}, u32[]{:S(2)}, u32[]{:S(2)}) %collective-permute-start.1) | collective-permute-done | bytes 1048608 | tf_op jit(solution)/shard_map/ppermute | solution.py:36
  31.5 2.6 %collective-permute-done.refs_2_.refs_6_ = bf16[8,128,512]{2,1,0:T(8,128)(2,1)S(1)} collective-permute-done((bf16[8,128,512]{2,1,0:T(8,128)(2,1)}, bf16[8,128,512]{2,1,0:T(8,128)(2,1)S(1)}, u32[]{:S(2)}, u32[]{:S(2)}) %collective-permute-start) | collective-permute-done | bytes 1048608 | tf_op jit(solution)/shard_map/ppermute | solution.py:36
  34.2 17.8 %collective-permute-start.19 = (bf16[8,128,512]{2,1,0:T(8,128)(2,1)S(1)}, bf16[8,128,512]{2,1,0:T(8,128)(2,1)}, u32[]{:S(2)}, u32[]{:S(2)}) collective-permute-start(bf16[8,128,512]{2,1,0:T(8,128)(2,1)S(1)} %collective-permute-done.refs_2_.refs_6_), channel_id=1, source_target_pairs={{0,1},{1,2},{2,3},{3,4},{4,5},{5,6},{6,7},{7,0},{8,9},{9,10},{10,1... | collective-permute-start | bytes 3145736 | tf_op jit(solution)/shard_map/ppermute | solution.py:20
  55.7 12.9 %collective-permute-done.19.refs_6_ = bf16[8,128,512]{2,1,0:T(8,128)(2,1)} collective-permute-done((bf16[8,128,512]{2,1,0:T(8,128)(2,1)S(1)}, bf16[8,128,512]{2,1,0:T(8,128)(2,1)}, u32[]{:S(2)}, u32[]{:S(2)}) %collective-permute-start.19) | collective-permute-done | bytes 1048608 | tf_op jit(solution)/shard_map/ppermute | solution.py:20
  70.2 9.9 %collective-permute-done.8 = f32[8,512]{1,0:T(8,128)S(1)} collective-permute-done((f32[8,512]{1,0:T(8,128)}, f32[8,512]{1,0:T(8,128)S(1)}, u32[]{:S(2)}, u32[]{:S(2)}) %collective-permute-start.8) | collective-permute-done | bytes 16416 | tf_op jit(solution)/shard_map/ppermute | solution.py:15
  81.3 4.7 %collective-permute-done.9 = f32[8,512]{1,0:T(8,128)S(1)} collective-permute-done((f32[8,512]{1,0:T(8,128)}, f32[8,512]{1,0:T(8,128)S(1)}, u32[]{:S(2)}, u32[]{:S(2)}) %collective-permute-start.9) | collective-permute-done | bytes 16416 | tf_op jit(solution)/shard_map/ppermute | solution.py:15
  86.7 32.9 %collective-permute-start.10 = (f32[8,2048]{1,0:T(8,128)S(1)}, f32[8,2048]{1,0:T(8,128)S(1)}, u32[]{:S(2)}, u32[]{:S(2)}) collective-permute-start(f32[8,2048]{1,0:T(8,128)S(1)} %pad_maximum_fusion), channel_id=1, source_target_pairs={{0,1},{1,0},{2,3},{3,2},{4,5},{5,4},{6,7},{7,6},{8,9},{9,8},{10,11... | collective-permute-start | bytes 196616 | tf_op jit(solution)/shard_map/ppermute | solution.py:15
  121.2 4.2 %gather_fusion = f32[2560,8]{1,0:T(8,128)S(1)} fusion(f32[8,4096]{0,1:T(8,128)S(1)} %copy.18, s32[3072]{0:T(1024)S(1)} %pad_clamp_fusion), kind=kCustom, calls=%fused_computation | custom fusion | bytes 174080 | tf_op jit(solution)/shard_map/jit(_take)/gather | solution.py:255
  126.9 9.1 %collective-permute-done.4.refs_8_ = bf16[8,128,512]{2,1,0:T(8,128)(2,1)} collective-permute-done((bf16[8,128,512]{2,1,0:T(8,128)(2,1)}, bf16[8,128,512]{2,1,0:T(8,128)(2,1)}, u32[]{:S(2)}, u32[]{:S(2)}) %collective-permute-start.4) | collective-permute-done | bytes 1048608 | tf_op jit(solution)/shard_map/ppermute | solution.py:20
  138.0 10.9 %shard_map.41.refs_11_ = bf16[8,5,512,1024]{3,2,1,0:T(8,128)(2,1)} custom-call(s32[8]{0:T(128)} %stack.38.refs_0_, bf16[8,128,512]{2,1,0:T(8,128)(2,1)} %shard_map.37.refs_1_.refs_5_, bf16[8,128,512]{2,1,0:T(8,128)(2,1)} %copy-done.1, bf16[8,128,512]{2,1,0:T(8,128)(2,1)} %copy-done, bf16[8,128,512]{2,1,0:T(8,128)(2,1)} %copy-done.2, ...), custom_call_target="tpu_custom_call" | custom-call | flops 4294967296 | bytes 16777216 | tf_op jit(solution)/shard_map/pallas_call | solution.py:183
  149.0 9.5 %collective-permute-done.21.refs_6_ = bf16[8,128,512]{2,1,0:T(8,128)(2,1)} collective-permute-done((bf16[8,128,512]{2,1,0:T(8,128)(2,1)}, bf16[8,128,512]{2,1,0:T(8,128)(2,1)}, u32[]{:S(2)}, u32[]{:S(2)}) %collective-permute-start.21) | collective-permute-done | bytes 1048608 | tf_op jit(solution)/shard_map/ppermute | solution.py:20
  158.5 10.4 %shard_map.42.refs_11_ = bf16[8,5,512,1024]{3,2,1,0:T(8,128)(2,1)} custom-call(s32[8]{0:T(128)} %stack.41.refs_0_, bf16[8,128,512]{2,1,0:T(8,128)(2,1)} %shard_map.37.refs_1_.refs_5_, bf16[8,128,512]{2,1,0:T(8,128)(2,1)} %copy-done.1, bf16[8,128,512]{2,1,0:T(8,128)(2,1)} %copy-done, bf16[8,128,512]{2,1,0:T(8,128)(2,1)} %copy-done.2, ...), custom_call_target="tpu_custom_call", output_to_operand_aliasing={{}: (11, {})} | custom-call | flops 4294967296 | bytes 16777216 | tf_op jit(solution)/shard_map/pallas_call | solution.py:183
  169.8 10.4 %shard_map.43.refs_8_ = bf16[8,5,512,1024]{3,2,1,0:T(8,128)(2,1)} custom-call(s32[8]{0:T(128)} %stack.38.refs_0_, bf16[8,128,512]{2,1,0:T(8,128)(2,1)} %shard_map.37.refs_1_.refs_5_, bf16[8,128,512]{2,1,0:T(8,128)(2,1)} %copy-done.1, bf16[8,128,512]{2,1,0:T(8,128)(2,1)} %copy-done, bf16[8,128,512]{2,1,0:T(8,128)(2,1)} %copy-done.2, ...), custom_call_target="tpu_custom_call", output_to_operand_aliasing={{}: (11, {})} | custom-call | flops 4294967296 | bytes 16777216 | tf_op jit(solution)/shard_map/pallas_call | solution.py:183
  183.3 9.0 %collective-permute-done.23.refs_5_ = bf16[8,128,512]{2,1,0:T(8,128)(2,1)} collective-permute-done((bf16[8,128,512]{2,1,0:T(8,128)(2,1)}, bf16[8,128,512]{2,1,0:T(8,128)(2,1)}, u32[]{:S(2)}, u32[]{:S(2)}) %collective-permute-start.23) | collective-permute-done | bytes 1048608 | tf_op jit(solution)/shard_map/ppermute | solution.py:20
  192.2 6.0 %shard_map.44.refs_8_ = bf16[8,5,512,1024]{3,2,1,0:T(8,128)(2,1)} custom-call(s32[8]{0:T(128)} %stack.38.refs_0_, bf16[8,128,512]{2,1,0:T(8,128)(2,1)} %shard_map.37.refs_1_.refs_5_, bf16[8,128,512]{2,1,0:T(8,128)(2,1)} %copy-done.1, bf16[8,128,512]{2,1,0:T(8,128)(2,1)} %copy-done, bf16[8,128,512]{2,1,0:T(8,128)(2,1)} %copy-done.2, ...), custom_call_target="tpu_custom_call", output_to_operand_aliasing={{}: (8, {})} | custom-call | flops 1073741824 | bytes 10485760 | tf_op jit(solution)/shard_map/pallas_call | solution.py:183
  198.2 5.3 %collective-permute-done.22.refs_5_ = bf16[8,128,512]{2,1,0:T(8,128)(2,1)} collective-permute-done((bf16[8,128,512]{2,1,0:T(8,128)(2,1)}, bf16[8,128,512]{2,1,0:T(8,128)(2,1)}, u32[]{:S(2)}, u32[]{:S(2)}) %collective-permute-start.22) | collective-permute-done | bytes 1048608 | tf_op jit(solution)/shard_map/ppermute | solution.py:20
  203.5 6.0 %shard_map.45.refs_11_ = bf16[8,5,512,1024]{3,2,1,0:T(8,128)(2,1)} custom-call(s32[8]{0:T(128)} %stack.38.refs_0_, bf16[8,128,512]{2,1,0:T(8,128)(2,1)} %shard_map.37.refs_1_.refs_5_, bf16[8,128,512]{2,1,0:T(8,128)(2,1)} %copy-done.1, bf16[8,128,512]{2,1,0:T(8,128)(2,1)} %copy-done, bf16[8,128,512]{2,1,0:T(8,128)(2,1)} %copy-done.2, ...), custom_call_target="tpu_custom_call", output_to_operand_aliasing={{}: (8, {})} | custom-call | flops 1073741824 | bytes 10485760 | tf_op jit(solution)/shard_map/pallas_call | solution.py:183
  209.4 10.4 %shard_map.46.refs_8_ = bf16[8,5,512,1024]{3,2,1,0:T(8,128)(2,1)} custom-call(s32[8]{0:T(128)} %stack.41.refs_0_, bf16[8,128,512]{2,1,0:T(8,128)(2,1)} %shard_map.37.refs_1_.refs_5_, bf16[8,128,512]{2,1,0:T(8,128)(2,1)} %copy-done.1, bf16[8,128,512]{2,1,0:T(8,128)(2,1)} %copy-done, bf16[8,128,512]{2,1,0:T(8,128)(2,1)} %copy-done.2, ...), custom_call_target="tpu_custom_call", output_to_operand_aliasing={{}: (11, {})} | custom-call | flops 4294967296 | bytes 16777216 | tf_op jit(solution)/shard_map/pallas_call | solution.py:183
  219.8 6.0 %shard_map.47.refs_8_ = bf16[8,5,512,1024]{3,2,1,0:T(8,128)(2,1)} custom-call(s32[8]{0:T(128)} %stack.38.refs_0_, bf16[8,128,512]{2,1,0:T(8,128)(2,1)} %shard_map.37.refs_1_.refs_5_, bf16[8,128,512]{2,1,0:T(8,128)(2,1)} %copy-done.1, bf16[8,128,512]{2,1,0:T(8,128)(2,1)} %copy-done, bf16[8,128,512]{2,1,0:T(8,128)(2,1)} %copy-done.2, ...), custom_call_target="tpu_custom_call", output_to_operand_aliasing={{}: (8, {})} | custom-call | flops 1073741824 | bytes 10485760 | tf_op jit(solution)/shard_map/pallas_call | solution.py:183
  225.8 4.3 %shard_map.48.refs_8_ = bf16[8,5,512,1024]{3,2,1,0:T(8,128)(2,1)} custom-call(s32[8]{0:T(128)} %stack.38.refs_0_, bf16[8,128,512]{2,1,0:T(8,128)(2,1)} %shard_map.37.refs_1_.refs_5_, bf16[8,128,512]{2,1,0:T(8,128)(2,1)} %copy-done.1, bf16[8,128,512]{2,1,0:T(8,128)(2,1)} %copy-done, bf16[8,128,512]{2,1,0:T(8,128)(2,1)} %copy-done.2, ...), custom_call_target="tpu_custom_call", output_to_operand_aliasing={{}: (8, {})} | custom-call | flops 536870912 | bytes 5242880 | tf_op jit(solution)/shard_map/pallas_call | solution.py:183
  230.1 4.3 %shard_map.49 = bf16[8,5,512,1024]{3,2,1,0:T(8,128)(2,1)} custom-call(s32[8]{0:T(128)} %stack.38.refs_0_, bf16[8,128,512]{2,1,0:T(8,128)(2,1)} %shard_map.37.refs_1_.refs_5_, bf16[8,128,512]{2,1,0:T(8,128)(2,1)} %copy-done.1, bf16[8,128,512]{2,1,0:T(8,128)(2,1)} %copy-done, bf16[8,128,512]{2,1,0:T(8,128)(2,1)} %copy-done.2, ...), custom_call_target="tpu_custom_call", output_to_operand_aliasing={{}: (8, {})} | custom-call | flops 536870912 | bytes 5242880 | tf_op jit(solution)/shard_map/pallas_call | solution.py:183
  (61 shorter events, 23.7 us)
Async XLA Ops:
  2.5 28.1 %collective-permute-start.1 = (bf16[8,128,512]{2,1,0:T(8,128)(2,1)}, bf16[8,128,512]{2,1,0:T(8,128)(2,1)S(1)}, u32[]{:S(2)}, u32[]{:S(2)}) collective-permute-start(bf16[8,128,512]{2,1,0:T(8,128)(2,1)} %shard_map.39), channel_id=1, source_target_pairs={{0,16},{1,9},{2,18},{3,11},{4,20},{5,13},{6,22},{7,15},{8,24},{9,1... | collective-permute-start | bytes 3145736 | tf_op jit(solution)/shard_map/ppermute | solution.py:36
  7.9 26.2 %collective-permute-start = (bf16[8,128,512]{2,1,0:T(8,128)(2,1)}, bf16[8,128,512]{2,1,0:T(8,128)(2,1)S(1)}, u32[]{:S(2)}, u32[]{:S(2)}) collective-permute-start(bf16[8,128,512]{2,1,0:T(8,128)(2,1)} %shard_map.38), channel_id=1, source_target_pairs={{0,8},{1,17},{2,10},{3,19},{4,12},{5,21},{6,14},{7,23},{8,0},{9,25... | collective-permute-start | bytes 3145736 | tf_op jit(solution)/shard_map/ppermute | solution.py:36
  11.8 40.6 %collective-permute-start.2 = (bf16[8,128,512]{2,1,0:T(8,128)(2,1)}, bf16[8,128,512]{2,1,0:T(8,128)(2,1)S(1)}, u32[]{:S(2)}, u32[]{:S(2)}) collective-permute-start(bf16[8,128,512]{2,1,0:T(8,128)(2,1)} %shard_map.40), channel_id=1, source_target_pairs={{0,24},{1,25},{2,26},{3,27},{4,28},{5,29},{6,30},{7,31},{8,16},{9,... | collective-permute-start | bytes 3145736 | tf_op jit(solution)/shard_map/ppermute | solution.py:36
  14.3 40.0 %collective-permute-start.16 = (bf16[8,128,512]{2,1,0:T(8,128)(2,1)}, bf16[8,128,512]{2,1,0:T(8,128)(2,1)}, u32[]{:S(2)}, u32[]{:S(2)}) collective-permute-start(bf16[8,128,512]{2,1,0:T(8,128)(2,1)} %shard_map.37.refs_1_.refs_5_), channel_id=1, source_target_pairs={{0,1},{1,2},{2,3},{3,4},{4,5},{5,6},{6,7},{7,0},{8,9},{9,10},{10,1... | collective-permute-start | bytes 3145736 | tf_op jit(solution)/shard_map/ppermute | solution.py:20
  31.5 24.1 %collective-permute-start.12 = (bf16[8,128,512]{2,1,0:T(8,128)(2,1)S(1)}, bf16[8,128,512]{2,1,0:T(8,128)(2,1)}, u32[]{:S(2)}, u32[]{:S(2)}) collective-permute-start(bf16[8,128,512]{2,1,0:T(8,128)(2,1)S(1)} %collective-permute-done.1.refs_3_.refs_7_), channel_id=1, source_target_pairs={{0,1},{1,2},{2,3},{3,4},{4,5},{5,6},{6,7},{7,0},{8,9},{9,10},{10,1... | collective-permute-start | bytes 3145736 | tf_op jit(solution)/shard_map/ppermute | solution.py:20
  34.2 34.4 %collective-permute-start.19 = (bf16[8,128,512]{2,1,0:T(8,128)(2,1)S(1)}, bf16[8,128,512]{2,1,0:T(8,128)(2,1)}, u32[]{:S(2)}, u32[]{:S(2)}) collective-permute-start(bf16[8,128,512]{2,1,0:T(8,128)(2,1)S(1)} %collective-permute-done.refs_2_.refs_6_), channel_id=1, source_target_pairs={{0,1},{1,2},{2,3},{3,4},{4,5},{5,6},{6,7},{7,0},{8,9},{9,10},{10,1... | collective-permute-start | bytes 3145736 | tf_op jit(solution)/shard_map/ppermute | solution.py:20
  52.5 67.2 %collective-permute-start.3 = (bf16[8,128,512]{2,1,0:T(8,128)(2,1)S(1)}, bf16[8,128,512]{2,1,0:T(8,128)(2,1)}, u32[]{:S(2)}, u32[]{:S(2)}) collective-permute-start(bf16[8,128,512]{2,1,0:T(8,128)(2,1)S(1)} %collective-permute-done.2.refs_4_.refs_8_), channel_id=1, source_target_pairs={{0,1},{1,2},{2,3},{3,4},{4,5},{5,6},{6,7},{7,0},{8,9},{9,10},{10,1... | collective-permute-start | bytes 3145736 | tf_op jit(solution)/shard_map/ppermute | solution.py:20
  52.5 16.9 %collective-permute-start.7 = (f32[8,512]{1,0:T(8,128)}, f32[8,512]{1,0:T(8,128)S(1)}, u32[]{:S(2)}, u32[]{:S(2)}) collective-permute-start(f32[8,512]{1,0:T(8,128)} %param.4), channel_id=1, source_target_pairs={{0,2},{1,3},{2,0},{3,1},{4,6},{5,7},{6,4},{7,5},{8,10},{9,11},{10,... | collective-permute-start | bytes 49160 | tf_op jit(solution)/shard_map/ppermute | solution.py:15
  54.3 71.4 %collective-permute-start.17 = (bf16[8,128,512]{2,1,0:T(8,128)(2,1)}, bf16[8,128,512]{2,1,0:T(8,128)(2,1)}, u32[]{:S(2)}, u32[]{:S(2)}) collective-permute-start(bf16[8,128,512]{2,1,0:T(8,128)(2,1)} %collective-permute-done.16.refs_5_), channel_id=1, source_target_pairs={{0,1},{1,2},{2,3},{3,4},{4,5},{5,6},{6,7},{7,0},{8,9},{9,10},{10,1... | collective-permute-start | bytes 3145736 | tf_op jit(solution)/shard_map/ppermute | solution.py:20
  55.7 70.5 %collective-permute-start.13 = (bf16[8,128,512]{2,1,0:T(8,128)(2,1)}, bf16[8,128,512]{2,1,0:T(8,128)(2,1)}, u32[]{:S(2)}, u32[]{:S(2)}) collective-permute-start(bf16[8,128,512]{2,1,0:T(8,128)(2,1)} %collective-permute-done.12.refs_7_), channel_id=1, source_target_pairs={{0,1},{1,2},{2,3},{3,4},{4,5},{5,6},{6,7},{7,0},{8,9},{9,10},{10,1... | collective-permute-start | bytes 3145736 | tf_op jit(solution)/shard_map/ppermute | solution.py:20
  68.6 57.5 %collective-permute-start.20 = (bf16[8,128,512]{2,1,0:T(8,128)(2,1)}, bf16[8,128,512]{2,1,0:T(8,128)(2,1)}, u32[]{:S(2)}, u32[]{:S(2)}) collective-permute-start(bf16[8,128,512]{2,1,0:T(8,128)(2,1)} %collective-permute-done.19.refs_6_), channel_id=1, source_target_pairs={{0,1},{1,2},{2,3},{3,4},{4,5},{5,6},{6,7},{7,0},{8,9},{9,10},{10,1... | collective-permute-start | bytes 3145736 | tf_op jit(solution)/shard_map/ppermute | solution.py:20
  69.3 10.8 %collective-permute-start.8 = (f32[8,512]{1,0:T(8,128)}, f32[8,512]{1,0:T(8,128)S(1)}, u32[]{:S(2)}, u32[]{:S(2)}) collective-permute-start(f32[8,512]{1,0:T(8,128)} %param.4), channel_id=1, source_target_pairs={{0,4},{1,5},{2,6},{3,7},{4,0},{5,1},{6,2},{7,3},{8,12},{9,13},{10,... | collective-permute-start | bytes 49160 | tf_op jit(solution)/shard_map/ppermute | solution.py:15
  80.1 5.9 %collective-permute-start.9 = (f32[8,512]{1,0:T(8,128)}, f32[8,512]{1,0:T(8,128)S(1)}, u32[]{:S(2)}, u32[]{:S(2)}) collective-permute-start(f32[8,512]{1,0:T(8,128)} %param.4), channel_id=1, source_target_pairs={{0,6},{1,7},{2,4},{3,5},{4,2},{5,3},{6,0},{7,1},{8,14},{9,15},{10,... | collective-permute-start | bytes 49160 | tf_op jit(solution)/shard_map/ppermute | solution.py:15
  86.7 33.8 %collective-permute-start.10 = (f32[8,2048]{1,0:T(8,128)S(1)}, f32[8,2048]{1,0:T(8,128)S(1)}, u32[]{:S(2)}, u32[]{:S(2)}) collective-permute-start(f32[8,2048]{1,0:T(8,128)S(1)} %pad_maximum_fusion), channel_id=1, source_target_pairs={{0,1},{1,0},{2,3},{3,2},{4,5},{5,4},{6,7},{7,6},{8,9},{9,8},{10,11... | collective-permute-start | bytes 196616 | tf_op jit(solution)/shard_map/ppermute | solution.py:15
  119.7 16.4 %collective-permute-start.4 = (bf16[8,128,512]{2,1,0:T(8,128)(2,1)}, bf16[8,128,512]{2,1,0:T(8,128)(2,1)}, u32[]{:S(2)}, u32[]{:S(2)}) collective-permute-start(bf16[8,128,512]{2,1,0:T(8,128)(2,1)} %collective-permute-done.3.refs_8_), channel_id=1, source_target_pairs={{0,1},{1,2},{2,3},{3,4},{4,5},{5,6},{6,7},{7,0},{8,9},{9,10},{10,1... | collective-permute-start | bytes 3145736 | tf_op jit(solution)/shard_map/ppermute | solution.py:20
  125.7 23.3 %collective-permute-start.18 = (bf16[8,128,512]{2,1,0:T(8,128)(2,1)}, bf16[8,128,512]{2,1,0:T(8,128)(2,1)}, u32[]{:S(2)}, u32[]{:S(2)}) collective-permute-start(bf16[8,128,512]{2,1,0:T(8,128)(2,1)} %collective-permute-done.17.refs_5_), channel_id=1, source_target_pairs={{0,1},{1,2},{2,3},{3,4},{4,5},{5,6},{6,7},{7,0},{8,9},{9,10},{10,1... | collective-permute-start | bytes 3145736 | tf_op jit(solution)/shard_map/ppermute | solution.py:20
  126.1 32.4 %collective-permute-start.21 = (bf16[8,128,512]{2,1,0:T(8,128)(2,1)}, bf16[8,128,512]{2,1,0:T(8,128)(2,1)}, u32[]{:S(2)}, u32[]{:S(2)}) collective-permute-start(bf16[8,128,512]{2,1,0:T(8,128)(2,1)} %collective-permute-done.20.refs_6_), channel_id=1, source_target_pairs={{0,1},{1,2},{2,3},{3,4},{4,5},{5,6},{6,7},{7,0},{8,9},{9,10},{10,1... | collective-permute-start | bytes 3145736 | tf_op jit(solution)/shard_map/ppermute | solution.py:20
  126.2 43.6 %collective-permute-start.14 = (bf16[8,128,512]{2,1,0:T(8,128)(2,1)}, bf16[8,128,512]{2,1,0:T(8,128)(2,1)}, u32[]{:S(2)}, u32[]{:S(2)}) collective-permute-start(bf16[8,128,512]{2,1,0:T(8,128)(2,1)} %collective-permute-done.13.refs_7_), channel_id=1, source_target_pairs={{0,1},{1,2},{2,3},{3,4},{4,5},{5,6},{6,7},{7,0},{8,9},{9,10},{10,1... | collective-permute-start | bytes 3145736 | tf_op jit(solution)/shard_map/ppermute | solution.py:20
  136.1 44.9 %collective-permute-start.5 = (bf16[8,128,512]{2,1,0:T(8,128)(2,1)}, bf16[8,128,512]{2,1,0:T(8,128)(2,1)}, u32[]{:S(2)}, u32[]{:S(2)}) collective-permute-start(bf16[8,128,512]{2,1,0:T(8,128)(2,1)} %collective-permute-done.4.refs_8_), channel_id=1, source_target_pairs={{0,1},{1,2},{2,3},{3,4},{4,5},{5,6},{6,7},{7,0},{8,9},{9,10},{10,1... | collective-permute-start | bytes 3145736 | tf_op jit(solution)/shard_map/ppermute | solution.py:20
  149.0 43.3 %collective-permute-start.23 = (bf16[8,128,512]{2,1,0:T(8,128)(2,1)}, bf16[8,128,512]{2,1,0:T(8,128)(2,1)}, u32[]{:S(2)}, u32[]{:S(2)}) collective-permute-start(bf16[8,128,512]{2,1,0:T(8,128)(2,1)} %collective-permute-done.18.refs_5_), channel_id=1, source_target_pairs={{0,1},{1,2},{2,3},{3,4},{4,5},{5,6},{6,7},{7,0},{8,9},{9,10},{10,1... | collective-permute-start | bytes 3145736 | tf_op jit(solution)/shard_map/ppermute | solution.py:20
  158.5 44.9 %collective-permute-start.22 = (bf16[8,128,512]{2,1,0:T(8,128)(2,1)}, bf16[8,128,512]{2,1,0:T(8,128)(2,1)}, u32[]{:S(2)}, u32[]{:S(2)}) collective-permute-start(bf16[8,128,512]{2,1,0:T(8,128)(2,1)} %collective-permute-done.21.refs_6_), channel_id=1, source_target_pairs={{0,1},{1,2},{2,3},{3,4},{4,5},{5,6},{6,7},{7,0},{8,9},{9,10},{10,1... | collective-permute-start | bytes 3145736 | tf_op jit(solution)/shard_map/ppermute | solution.py:20
  169.8 50.1 %collective-permute-start.15 = (bf16[8,128,512]{2,1,0:T(8,128)(2,1)}, bf16[8,128,512]{2,1,0:T(8,128)(2,1)}, u32[]{:S(2)}, u32[]{:S(2)}) collective-permute-start(bf16[8,128,512]{2,1,0:T(8,128)(2,1)} %collective-permute-done.14.refs_7_), channel_id=1, source_target_pairs={{0,1},{1,2},{2,3},{3,4},{4,5},{5,6},{6,7},{7,0},{8,9},{9,10},{10,1... | collective-permute-start | bytes 3145736 | tf_op jit(solution)/shard_map/ppermute | solution.py:20
  183.3 42.5 %collective-permute-start.11 = (bf16[4,128,512]{2,1,0:T(8,128)(2,1)}, bf16[4,128,512]{2,1,0:T(8,128)(2,1)}, u32[]{:S(2)}, u32[]{:S(2)}) collective-permute-start(bf16[4,128,512]{2,1,0:T(8,128)(2,1)} %get-tuple-element.5), channel_id=1, source_target_pairs={{0,1},{1,2},{2,3},{3,4},{4,5},{5,6},{6,7},{7,0},{8,9},{9,10},{10,1... | collective-permute-start | bytes 1572872 | tf_op jit(solution)/shard_map/ppermute | solution.py:20
  183.3 46.8 %collective-permute-start.6 = (bf16[4,128,512]{2,1,0:T(8,128)(2,1)}, bf16[4,128,512]{2,1,0:T(8,128)(2,1)}, u32[]{:S(2)}, u32[]{:S(2)}) collective-permute-start(bf16[4,128,512]{2,1,0:T(8,128)(2,1)} %get-tuple-element.6), channel_id=1, source_target_pairs={{0,1},{1,2},{2,3},{3,4},{4,5},{5,6},{6,7},{7,0},{8,9},{9,10},{10,1... | collective-permute-start | bytes 1572872 | tf_op jit(solution)/shard_map/ppermute | solution.py:20
  (3 other events, 38.6 us)
